TPU v7x, 256 devices: a whole 4x4x8 slice. The times are simulated.
256 devices in a mesh: row: 8 (over y, x_lo), col: 32 (over x_hi, z, core).
Axes of the slice: x: 4 (x_hi: 2, x_lo: 2; x = x_hi * 2 + x_lo), y: 4, z: 8, core: 2. Of those that a mesh axis runs over, the one named last changes fastest.
Arguments:
- inverse_state: float32 [4, 2048, 1, 8192], P(None, 'row', None, 'col')
- row_seeds: int32 [2, 4, 2048], P(None, None, 'row'), may hold values from 0 to 31
- col_seeds: int32 [2, 1, 8192], P(None, None, 'col'), may hold values from 0 to 31
Outputs:
- inverse: float32 [4, 2048, 1, 8192], P(None, 'row', None, 'col')
All inputs are finite; a program needn't handle non-finite values.
Results may differ from a plain program's by a relative error of at most 0.0002.
Values sent between devices are 32-bit elements; how exact they have to be, the bound alone decides.
No kernel may reach another device: no remote copies, remote signals or barrier semaphores. Data moves between devices by JAX's collectives and lax.ppermute only.
A program may use at most 64 MiB of HBM per device.

v0:
```python
import jax
import jax.numpy as jnp
from jax import lax
from jax.sharding import PartitionSpec as P

STEPS = 2
root_half = 0.7071067811865476


def filled_up(lines, length):
    spare = -len(lines) % length
    return jnp.pad(lines, [(0, spare)] + [(0, 0)] * (lines.ndim - 1))


def from_root(x, axis, root):
    lines = jnp.where(lax.axis_index(axis) == root, x, jnp.zeros_like(x)).reshape(
        -1, *x.shape[1:][-1:]
    )
    padded = filled_up(lines, lax.axis_size(axis))
    own = lax.psum_scatter(padded, axis, scatter_dimension=0, tiled=True)
    return lax.all_gather(own, axis, axis=0, tiled=True)[: len(lines)].reshape(x.shape)


def broadcast(x, axis, root):
    return lax.dynamic_index_in_dim(lax.all_gather(x, axis), root, 0, keepdims=False)


def swapped(block, axis, bit):
    count = lax.axis_size(axis)
    route = []
    for low in range(count):
        high = low | 1 << bit
        if high != low and high < count:
            route += [(low, high), (high, low)]
    return lax.ppermute(block, axis, route)


def seed_values(seeds):
    return (2.0 * seeds.astype(jnp.float32) - 31.0) / 16.0


def row_level(matrix, scales, groups):
    count = matrix.shape[0]
    half = count // (2 * groups)
    shaped = matrix.reshape((groups, 2, half) + matrix.shape[1:])
    factor = scales.reshape((groups, 2, half, scales.shape[1]) + (1,) * (matrix.ndim - 2))
    upper = factor[:, 0] * shaped[:, 0]
    lower = factor[:, 1] * shaped[:, 1]
    return (jnp.stack([upper + lower, upper - lower], axis=1) * root_half).reshape(matrix.shape)


def row_butterfly(matrix, seeds):
    scales = seed_values(seeds)
    return row_level(row_level(matrix, scales[0], 1), scales[1], 2)


def col_level(matrix, scales, mover, col_index, span):
    own_part = scales * matrix
    partner = mover(own_part)
    on_top = col_index // span % 2 == 0
    return jnp.where(on_top, own_part + partner, partner - own_part) * root_half


def col_butterfly(matrix, seeds, first_mover, second_mover):
    scales = seed_values(seeds)
    col_count = lax.axis_size("col")
    col_index = lax.axis_index("col")
    blocks_all = matrix.shape[1] * col_count
    span_one = blocks_all // 2
    span_two = blocks_all // 4
    matrix = col_level(matrix, scales[0], first_mover, col_index, span_one)
    return col_level(matrix, scales[1], second_mover, col_index, span_two)


def solve_block(pivot, rows_given):
    gram = jnp.dot(
        pivot.T, pivot, precision=lax.Precision.HIGHEST, preferred_element_type=jnp.float32
    )
    factor = jnp.linalg.cholesky(gram)
    right_side = jnp.dot(
        pivot.T, rows_given, precision=lax.Precision.HIGHEST, preferred_element_type=jnp.float32
    )
    middle = lax.linalg.triangular_solve(factor, right_side, left_side=True, lower=True)
    return lax.linalg.triangular_solve(factor, middle, left_side=True, lower=True, transpose_a=True)


def pivot_pieces(state, step):
    row_blocks = state.shape[0]
    block = state.shape[1]
    col_blocks = state.shape[2]
    row_count = lax.axis_size("row")
    col_count = lax.axis_size("col")
    target = row_blocks * row_count - STEPS + step
    row_root = target % row_count
    row_local = target // row_count
    col_root = target % col_count
    col_local = target // col_count
    on_row = lax.axis_index("row") == row_root
    on_col = lax.axis_index("col") == col_root
    identity = jnp.eye(block, dtype=jnp.float32)
    column = from_root(state[:, :, col_local, :], "col", col_root)
    pivot = jnp.where(on_row, column[row_local], identity)
    left_part = column.at[row_local].set(jnp.where(on_row, pivot - identity, column[row_local]))
    last_column = jnp.where(on_col, 0.0, state[:, :, col_local, :])
    last_column = last_column.at[row_local].set(
        jnp.where(on_row & on_col, identity, last_column[row_local])
    )
    shifted = state.at[:, :, col_local, :].set(last_column)
    pivot_rows = shifted[row_local].reshape(block, col_blocks * block)
    rows_there, pivot_there = (
        broadcast(pivot_rows, "row", row_root),
        broadcast(pivot, "row", row_root),
    )
    right_part = solve_block(pivot_there, rows_there)
    return (shifted, left_part, right_part)


def apply_update(shifted, left_part, right_part):
    row_blocks, block, col_blocks, _ = shifted.shape
    flat_left = left_part.reshape(row_blocks * block, block)
    update = shifted.reshape(row_blocks * block, col_blocks * block) - jnp.dot(
        flat_left, right_part, precision=lax.Precision.HIGHEST, preferred_element_type=jnp.float32
    )
    return update.reshape(shifted.shape)


def per_device(inverse_state, row_seeds, col_seeds):
    row_blocks = inverse_state.shape[0]
    block = inverse_state.shape[1]
    col_blocks = inverse_state.shape[2]
    col_count = lax.axis_size("col")
    state = inverse_state
    shifted, left_part, right_part = pivot_pieces(state, 0)
    state = apply_update(shifted, left_part, right_part)
    shifted, left_part, right_part = pivot_pieces(state, STEPS - 1)
    blocks_all = col_blocks * col_count
    bit_one = (blocks_all // 2).bit_length() - 1
    bit_two = (blocks_all // 4).bit_length() - 1
    moved = row_butterfly(shifted, row_seeds)
    moved = col_butterfly(
        moved.reshape(row_blocks * block, col_blocks, block),
        col_seeds,
        lambda values: swapped(values, "col", bit_one),
        lambda values: swapped(values, "col", bit_two),
    )
    left_moved = row_butterfly(left_part, row_seeds).reshape(row_blocks * block, block)
    right_moved = col_butterfly(
        right_part.reshape(block, col_blocks, block),
        col_seeds,
        lambda values: swapped(values, "col", bit_one),
        lambda values: swapped(values, "col", bit_two),
    )
    product = jnp.dot(
        left_moved,
        right_moved.reshape(block, col_blocks * block),
        precision=lax.Precision.HIGHEST,
        preferred_element_type=jnp.float32,
    )
    result = moved - product.reshape(moved.shape)
    return result.reshape(inverse_state.shape)


def solution(mesh):
    placed = (P(None, "row", None, "col"), P(None, None, "row"), P(None, None, "col"))
    return jax.shard_map(
        per_device,
        mesh=mesh,
        in_specs=placed,
        out_specs=P(None, "row", None, "col"),
        check_vma=False,
    )
```

profile of v0, /device:TPU:2, one launch (start us, length us, event | category | flops | bytes accessed | tf_op | source)
XLA Modules:
  0.0 705.1 jit_solution(6632455285220665631)
XLA Ops:
  6.5 2.4 copy_select_fusion
  9.0 120.5 %reduce-scatter.3.cloned.1.call-done = f32[32,256]{1,0:T(8,128)} async-done(((f32[1024,256]{1,0:T(8,128)}), f32[32,256]{1,0:T(8,128)}) %reduce-scatter.3.cloned.1.call-update) | async-done | bytes 32784 | tf_op jit(solution)/shard_map/reduce_scatter | solution.py:20
  129.6 78.4 %all-gather.9.cloned.1.call-done = f32[1024,256]{1,0:T(8,128)} async-done(((f32[32,256]{1,0:T(8,128)}), f32[1024,256]{1,0:T(8,128)}) %all-gather.9.cloned.1.call-update) | async-done | bytes 1048592 | tf_op jit(solution)/shard_map/all_gather | solution.py:21
  208.0 1.8 convert_select_fusion.1
  210.9 49.9 %all-gather.17.cloned.1.call-done = f32[2048,256]{1,0:T(8,128)} async-done(((f32[256,256]{1,0:T(8,128)}), f32[2048,256]{1,0:T(8,128)}) %all-gather.17.cloned.1.call-update) | async-done | bytes 2097168 | tf_op jit(solution)/shard_map/all_gather | solution.py:25
  260.8 1.6 fusion.30
  262.6 11.7 %cholesky.130 = f32[128,128]{1,0:T(8,128)S(1)} custom-call(f32[128,128]{1,0:T(8,128)S(1)} %cholesky.194), custom_call_target="Cholesky" | custom-call | tf_op jit(solution)/shard_map/jit(cholesky)/cholesky | solution.py:79
  274.3 9.8 %custom-call.17 = f32[1,128,128]{1,2,0:T(8,128)S(1)} custom-call(f32[1,128,128]{2,1,0:T(8,128)S(1)} %get-tuple-element.151), custom_call_target="InvertDiagBlocksLowerTriangular" | custom-call | tf_op jit(solution)/shard_map/jit(cholesky)/cholesky | solution.py:79
  284.7 11.7 %cholesky.147 = f32[128,128]{1,0:T(8,128)S(1)} custom-call(f32[128,128]{1,0:T(8,128)S(1)} %convolution_subtract_fusion.6), custom_call_target="Cholesky" | custom-call | tf_op jit(solution)/shard_map/jit(cholesky)/cholesky | solution.py:79
  298.4 4.3 while.14
  303.3 19.7 %custom-call.19 = f32[2,128,128]{1,2,0:T(8,128)S(1)} custom-call(f32[2,128,128]{2,1,0:T(8,128)S(1)} %get-tuple-element.109), custom_call_target="InvertDiagBlocksLowerTriangular" | custom-call | tf_op jit(solution)/shard_map/triangular_solve/custom-call.4 | solution.py:84
  323.0 1.6 fusion.13
  326.4 2.0 broadcast_select_fusion
  328.5 116.3 %reduce-scatter.5.cloned.1.call-done = f32[32,256]{1,0:T(8,128)} async-done(((f32[1024,256]{1,0:T(8,128)}), f32[32,256]{1,0:T(8,128)}) %reduce-scatter.5.cloned.1.call-update) | async-done | bytes 32784 | tf_op jit(solution)/shard_map/reduce_scatter | solution.py:20
  444.8 78.2 %all-gather.13.cloned.1.call-done = f32[1024,256]{1,0:T(8,128)} async-done(((f32[32,256]{1,0:T(8,128)}), f32[1024,256]{1,0:T(8,128)}) %all-gather.13.cloned.1.call-update) | async-done | bytes 1048592 | tf_op jit(solution)/shard_map/all_gather | solution.py:21
  523.1 1.7 convert_select_fusion
  526.8 1.4 collective-permute-start
  529.7 42.1 %collective-permute-done = f32[1024,1,256]{2,0,1:T(8,128)S(1)} collective-permute-done((f32[1024,1,256]{2,0,1:T(8,128)}, f32[1024,1,256]{2,0,1:T(8,128)S(1)}, u32[]{:S(2)}, u32[]{:S(2)}) %collective-permute-start) | collective-permute-done | bytes 1048608 | tf_op jit(solution)/shard_map/ppermute | solution.py:35
  572.8 1.4 select_multiply_fusion
  577.0 16.8 %all-gather.19.cloned.1.call-done = f32[2048,256]{1,0:T(8,128)} async-done(((f32[256,256]{1,0:T(8,128)}), f32[2048,256]{1,0:T(8,128)}) %all-gather.19.cloned.1.call-update) | async-done | bytes 2097168 | tf_op jit(solution)/shard_map/all_gather | solution.py:25
  593.8 1.6 fusion.27
  597.9 11.7 %cholesky.164 = f32[128,128]{1,0:T(8,128)S(1)} custom-call(f32[128,128]{1,0:T(8,128)S(1)} %cholesky.197), custom_call_target="Cholesky" | custom-call | tf_op jit(solution)/shard_map/jit(cholesky)/cholesky | solution.py:79
  610.2 9.8 %custom-call.20 = f32[1,128,128]{1,2,0:T(8,128)S(1)} custom-call(f32[1,128,128]{2,1,0:T(8,128)S(1)} %get-tuple-element.147), custom_call_target="InvertDiagBlocksLowerTriangular" | custom-call | tf_op jit(solution)/shard_map/jit(cholesky)/cholesky | solution.py:79
  622.2 11.7 %cholesky.181 = f32[128,128]{1,0:T(8,128)S(1)} custom-call(f32[128,128]{1,0:T(8,128)S(1)} %convolution_subtract_fusion.5), custom_call_target="Cholesky" | custom-call | tf_op jit(solution)/shard_map/jit(cholesky)/cholesky | solution.py:79
  638.1 5.5 while.15
  644.2 20.5 %custom-call.22 = f32[2,128,128]{1,2,0:T(8,128)S(1)} custom-call(f32[2,128,128]{2,1,0:T(8,128)} %copy-done.4), custom_call_target="InvertDiagBlocksLowerTriangular" | custom-call | tf_op jit(solution)/shard_map/triangular_solve/custom-call.4 | solution.py:84
  664.8 1.6 fusion.12
  668.2 1.8 collective-permute-start.2
  671.0 7.0 collective-permute-done.2
  678.0 3.3 collective-permute-start.3
  681.6 13.4 %collective-permute-done.3 = f32[256,1,256]{2,0,1:T(8,128)S(1)} collective-permute-done((f32[256,1,256]{2,0,1:T(8,128)S(1)}, f32[256,1,256]{2,0,1:T(8,128)S(1)}, u32[]{:S(2)}, u32[]{:S(2)}) %collective-permute-start.3) | collective-permute-done | bytes 262176 | tf_op jit(solution)/shard_map/ppermute | solution.py:35
  696.0 2.0 copy.17
  (121 shorter events, 34.1 us)
Async XLA Ops:
  6.5 123.0 %reduce-scatter.3.cloned.1.call-start = ((), (), s32[]{:S(2)}) async-start(), calls=%async_computation.2 | async-start | bytes 1081344 | tf_op jit(solution)/shard_map/reduce_scatter | solution.py:20
  9.0 199.1 %all-gather.9.cloned.1.call-start = ((), (), s32[]{:S(2)}) async-start(), calls=%async_computation.3 | async-start | bytes 1081344 | tf_op jit(solution)/shard_map/all_gather | solution.py:21
  129.6 131.2 %all-gather.17.cloned.1.call-start = ((), (), s32[]{:S(2)}) async-start(), calls=%async_computation.8 | async-start | bytes 2359296 | tf_op jit(solution)/shard_map/all_gather | solution.py:25
  208.0 2.7 copy-start
  209.8 113.2 %all-gather.11.cloned.1.call-start = ((), (), s32[]{:S(2)}) async-start(), calls=%async_computation.4 | async-start | bytes 2359296 | tf_op jit(solution)/shard_map/all_gather | solution.py:25
  210.6 234.1 %reduce-scatter.5.cloned.1.call-start = ((), (), s32[]{:S(2)}) async-start(), calls=%async_computation.5 | async-start | bytes 1081344 | tf_op jit(solution)/shard_map/reduce_scatter | solution.py:20
  302.7 0.6 copy-start.7
  326.4 198.4 %copy-start.5 = (s32[2,4,256]{2,1,0:T(4,128)S(1)}, s32[2,4,256]{2,1,0:T(4,128)}, u32[]{:S(2)}) copy-start(s32[2,4,256]{2,1,0:T(4,128)} %param.21) | copy-start | bytes 24580
  326.4 198.5 %copy-start.6 = (s32[2,1,256]{2,1,0:T(1,128)S(1)}, s32[2,1,256]{2,1,0:T(1,128)}, u32[]{:S(2)}) copy-start(s32[2,1,256]{2,1,0:T(1,128)} %param.22) | copy-start | bytes 6148
  328.4 194.7 %all-gather.13.cloned.1.call-start = ((), (), s32[]{:S(2)}) async-start(), calls=%async_computation.6 | async-start | bytes 1081344 | tf_op jit(solution)/shard_map/all_gather | solution.py:21
  444.8 149.0 %all-gather.19.cloned.1.call-start = ((), (), s32[]{:S(2)}) async-start(), calls=%async_computation.9 | async-start | bytes 2359296 | tf_op jit(solution)/shard_map/all_gather | solution.py:25
  524.8 140.0 %all-gather.15.cloned.1.call-start = ((), (), s32[]{:S(2)}) async-start(), calls=%async_computation.7 | async-start | bytes 2359296 | tf_op jit(solution)/shard_map/all_gather | solution.py:25
  526.8 45.0 %collective-permute-start = (f32[1024,1,256]{2,0,1:T(8,128)}, f32[1024,1,256]{2,0,1:T(8,128)S(1)}, u32[]{:S(2)}, u32[]{:S(2)}) collective-permute-start(f32[1024,1,256]{2,0,1:T(8,128)} %bitcast_multiply_fusion), channel_id=1, source_target_pairs={{0,16},{16,0},{1,17},{17,1},{2,18},{18,2},{3,19},{19,3},{4,20},{20... | collective-permute-start | bytes 3145736 | tf_op jit(solution)/shard_map/ppermute | solution.py:35
  571.8 1.0 copy-start.1
  574.2 107.4 %collective-permute-start.1 = (f32[1024,1,256]{2,0,1:T(8,128)S(1)}, f32[1024,1,256]{2,0,1:T(8,128)S(1)}, u32[]{:S(2)}, u32[]{:S(2)}) collective-permute-start(f32[1024,1,256]{2,0,1:T(8,128)S(1)} %select_multiply_fusion), channel_id=1, source_target_pairs={{0,8},{8,0},{1,9},{9,1},{2,10},{10,2},{3,11},{11,3},{4,12},{12,4},... | collective-permute-start | bytes 3145736 | tf_op jit(solution)/shard_map/ppermute | solution.py:35
  597.2 0.7 copy-start.3
  634.0 3.1 copy-start.2
  643.6 0.7 copy-start.4
  668.2 9.7 %collective-permute-start.2 = (f32[256,1,256]{2,0,1:T(8,128)S(1)}, f32[256,1,256]{2,0,1:T(8,128)S(1)}, u32[]{:S(2)}, u32[]{:S(2)}) collective-permute-start(f32[256,1,256]{2,0,1:T(8,128)S(1)} %fusion.17), channel_id=1, source_target_pairs={{0,16},{16,0},{1,17},{17,1},{2,18},{18,2},{3,19},{19,3},{4,20},{20... | collective-permute-start | bytes 786440 | tf_op jit(solution)/shard_map/ppermute | solution.py:35
  678.0 17.0 %collective-permute-start.3 = (f32[256,1,256]{2,0,1:T(8,128)S(1)}, f32[256,1,256]{2,0,1:T(8,128)S(1)}, u32[]{:S(2)}, u32[]{:S(2)}) collective-permute-start(f32[256,1,256]{2,0,1:T(8,128)S(1)} %select_multiply_fusion.1), channel_id=1, source_target_pairs={{0,8},{8,0},{1,9},{9,1},{2,10},{10,2},{3,11},{11,3},{4,12},{12,4},... | collective-permute-start | bytes 786440 | tf_op jit(solution)/shard_map/ppermute | solution.py:35
Sparse Core Ops, SparseCore 0:
  11.4 118.0 reduce-scatter.2
  132.3 75.6 all-gather.8
  209.9 50.7 all-gather.16
  262.4 54.0 all-gather.10
  328.5 116.1 reduce-scatter.4
  447.4 75.6 all-gather.12
  524.9 68.8 all-gather.18
  595.6 50.4 all-gather.14
where the time goes:
time: 714 us; the launch traced here: 705 us
  waiting for transfers between devices  523 us (73%)
  other arithmetic  125 us (18%)
  local copies, waits for them, and re-layouts  17.2 us (2%)
  between operations  16.8 us (2%)
  matrix products  15.6 us (2%)
  starting transfers between devices  7.33 us (1%)
    reduce_scatter x2, waiting for transfers between devices, from_root(): own = lax.psum_scatter(padded, axis, scatter_dimension=0, tiled=True)  237 us
    all_gather x2, waiting for transfers between devices, from_root(): lax.all_gather(own, axis, axis=0, tiled=True)[:len(lines)].reshape(x.shape)  157 us
    another operation x13, other arithmetic, solve_block(): factor = jnp.linalg.cholesky(gram)  69.7 us
    all_gather x4, waiting for transfers between devices, broadcast(): lax.all_gather(x, axis)  66.7 us
    ppermute x4, waiting for transfers between devices, swapped(): return lax.ppermute(block, axis, route)  62.5 us
    another operation x5, other arithmetic, solve_block(): lax.linalg.triangular_solve(factor, middle, left_side=True, lower=True, t...  41.2 us
  transfers between devices with their start and end apart: 12, of which 9 were waited for; matrix products, arithmetic and copies ran while one was open for 20% of the time, Pallas kernels for 0%

commit v1 on v0

--- a/solution.py
+++ b/solution.py
@@ -18,7 +18,9 @@
     )
     padded = filled_up(lines, lax.axis_size(axis))
     own = lax.psum_scatter(padded, axis, scatter_dimension=0, tiled=True)
-    return lax.all_gather(own, axis, axis=0, tiled=True)[: len(lines)].reshape(x.shape)
+    return jnp.concatenate(
+        lax.all_to_all(jnp.stack([own] * lax.axis_size(axis)), axis, 0, 0), axis=0
+    )[: len(lines)].reshape(x.shape)
 
 
 def broadcast(x, axis, root):

time: 714 us -> 623 us (0.87)
  the two profiles are of different devices: /device:TPU:2 before, /device:TPU:36 now
where the time goes in v1:
time: 623 us; the launch traced here: 613 us
  waiting for transfers between devices  428 us (69%)
  other arithmetic  117 us (19%)
  starting transfers between devices  21.7 us (3%)
  between operations  16.9 us (3%)
  matrix products  15.1 us (2%)
  local copies, waits for them, and re-layouts  14.2 us (2%)
    reduce_scatter x2, waiting for transfers between devices, from_root(): own = lax.psum_scatter(padded, axis, scatter_dimension=0, tiled=True)  233 us
    all_gather x4, waiting for transfers between devices, broadcast(): lax.all_gather(x, axis)  73.1 us
    another operation x13, other arithmetic, solve_block(): factor = jnp.linalg.cholesky(gram)  68.6 us
    ppermute x4, waiting for transfers between devices, swapped(): return lax.ppermute(block, axis, route)  65.3 us
    all_to_all x2, waiting for transfers between devices, from_root(): lax.all_to_all(jnp.stack([own] * lax.axis_size(axis)), axis, 0, 0)  55.9 us
    another operation x5, other arithmetic, solve_block(): lax.linalg.triangular_solve(factor, middle, left_side=True, lower=True, t...  39.4 us
    all_to_all x2, starting transfers between devices, from_root(): lax.all_to_all(jnp.stack([own] * lax.axis_size(axis)), axis, 0, 0)  16.3 us
  transfers between devices with their start and end apart: 12, of which 9 were waited for; matrix products, arithmetic and copies ran while one was open for 21% of the time, Pallas kernels for 0%

profile of v1, /device:TPU:36, one launch (start us, length us, event | category | flops | bytes accessed | tf_op | source)
XLA Modules:
  0.0 613.4 jit_solution(17442196088689440005)
XLA Ops:
  6.5 2.4 copy_select_fusion
  9.0 119.3 %reduce-scatter.3.cloned.1.call-done = f32[32,256]{1,0:T(8,128)} async-done(((f32[1024,256]{1,0:T(8,128)}), f32[32,256]{1,0:T(8,128)}) %reduce-scatter.3.cloned.1.call-update) | async-done | bytes 32784 | tf_op jit(solution)/shard_map/reduce_scatter | solution.py:20
  128.2 1.8 stack.22
  130.1 8.1 %all-to-all-start = ((f32[32,32,256]{2,1,0:T(8,128)}), f32[32,32,256]{2,1,0:T(8,128)S(1)}, u32[]{:S(2)}, u32[]{:S(2)}) async-start(f32[32,32,256]{2,1,0:T(8,128)} %stack.22), calls=%async_computation.1 | async-start | bytes 2097152 | tf_op jit(solution)/shard_map/all_to_all | solution.py:22
  138.2 27.9 %all-to-all-done = f32[32,32,256]{2,1,0:T(8,128)S(1)} async-done(((f32[32,32,256]{2,1,0:T(8,128)}), f32[32,32,256]{2,1,0:T(8,128)S(1)}, u32[]{:S(2)}, u32[]{:S(2)}) %all-to-all-start) | async-done | bytes 1048608 | tf_op jit(solution)/shard_map/all_to_all | solution.py:22
  167.9 51.6 %all-gather.5.cloned.1.call-done = f32[8,256,256]{2,1,0:T(8,128)} async-done(((f32[1,256,256]{2,1,0:T(8,128)}), f32[8,256,256]{2,1,0:T(8,128)}) %all-gather.5.cloned.1.call-update) | async-done | bytes 2097168 | tf_op jit(solution)/shard_map/all_gather | solution.py:27
  219.5 1.6 fusion.25
  221.3 11.7 %cholesky.130 = f32[128,128]{1,0:T(8,128)S(1)} custom-call(f32[128,128]{1,0:T(8,128)S(1)} %cholesky.194), custom_call_target="Cholesky" | custom-call | tf_op jit(solution)/shard_map/jit(cholesky)/cholesky | solution.py:81
  233.1 9.8 %custom-call.17 = f32[1,128,128]{1,2,0:T(8,128)S(1)} custom-call(f32[1,128,128]{2,1,0:T(8,128)S(1)} %get-tuple-element.155), custom_call_target="InvertDiagBlocksLowerTriangular" | custom-call | tf_op jit(solution)/shard_map/jit(cholesky)/cholesky | solution.py:81
  243.4 11.7 %cholesky.147 = f32[128,128]{1,0:T(8,128)S(1)} custom-call(f32[128,128]{1,0:T(8,128)S(1)} %convolution_subtract_fusion.6), custom_call_target="Cholesky" | custom-call | tf_op jit(solution)/shard_map/jit(cholesky)/cholesky | solution.py:81
  257.3 4.5 while.14
  261.8 19.7 %custom-call.19 = f32[2,128,128]{1,2,0:T(8,128)S(1)} custom-call(f32[2,128,128]{2,1,0:T(8,128)S(1)} %get-tuple-element.109), custom_call_target="InvertDiagBlocksLowerTriangular" | custom-call | tf_op jit(solution)/shard_map/triangular_solve/custom-call.4 | solution.py:86
  281.5 1.6 fusion.11
  284.9 2.0 broadcast_select_fusion
  286.9 113.9 %reduce-scatter.5.cloned.1.call-done = f32[32,256]{1,0:T(8,128)} async-done(((f32[1024,256]{1,0:T(8,128)}), f32[32,256]{1,0:T(8,128)}) %reduce-scatter.5.cloned.1.call-update) | async-done | bytes 32784 | tf_op jit(solution)/shard_map/reduce_scatter | solution.py:20
  400.8 1.8 stack.28
  402.7 8.2 %all-to-all-start.1 = ((f32[32,32,256]{2,1,0:T(8,128)}), f32[32,32,256]{2,1,0:T(8,128)S(1)}, u32[]{:S(2)}, u32[]{:S(2)}) async-start(f32[32,32,256]{2,1,0:T(8,128)} %stack.28), calls=%async_computation.3 | async-start | bytes 2097152 | tf_op jit(solution)/shard_map/all_to_all | solution.py:22
  411.0 27.9 %all-to-all-done.1 = f32[32,32,256]{2,1,0:T(8,128)S(1)} async-done(((f32[32,32,256]{2,1,0:T(8,128)}), f32[32,32,256]{2,1,0:T(8,128)S(1)}, u32[]{:S(2)}, u32[]{:S(2)}) %all-to-all-start.1) | async-done | bytes 1048608 | tf_op jit(solution)/shard_map/all_to_all | solution.py:22
  441.7 3.0 collective-permute-start
  445.6 41.2 %collective-permute-done = f32[1024,1,256]{2,0,1:T(8,128)} collective-permute-done((f32[1024,1,256]{2,0,1:T(8,128)}, f32[1024,1,256]{2,0,1:T(8,128)}, u32[]{:S(2)}, u32[]{:S(2)}) %collective-permute-start) | collective-permute-done | bytes 1048608 | tf_op jit(solution)/shard_map/ppermute | solution.py:37
  488.5 21.5 %all-gather.9.cloned.1.call-done = f32[8,256,256]{2,1,0:T(8,128)} async-done(((f32[1,256,256]{2,1,0:T(8,128)}), f32[8,256,256]{2,1,0:T(8,128)}) %all-gather.9.cloned.1.call-update) | async-done | bytes 2097168 | tf_op jit(solution)/shard_map/all_gather | solution.py:27
  511.8 11.7 %cholesky.164 = f32[128,128]{1,0:T(8,128)S(1)} custom-call(f32[128,128]{1,0:T(8,128)S(1)} %cholesky.197), custom_call_target="Cholesky" | custom-call | tf_op jit(solution)/shard_map/jit(cholesky)/cholesky | solution.py:81
  523.5 9.8 %custom-call.20 = f32[1,128,128]{1,2,0:T(8,128)S(1)} custom-call(f32[1,128,128]{2,1,0:T(8,128)S(1)} %get-tuple-element.151), custom_call_target="InvertDiagBlocksLowerTriangular" | custom-call | tf_op jit(solution)/shard_map/jit(cholesky)/cholesky | solution.py:81
  533.9 11.7 %cholesky.181 = f32[128,128]{1,0:T(8,128)S(1)} custom-call(f32[128,128]{1,0:T(8,128)S(1)} %convolution_subtract_fusion.5), custom_call_target="Cholesky" | custom-call | tf_op jit(solution)/shard_map/jit(cholesky)/cholesky | solution.py:81
  548.2 4.1 while.15
  552.3 19.7 %custom-call.22 = f32[2,128,128]{1,2,0:T(8,128)S(1)} custom-call(f32[2,128,128]{2,1,0:T(8,128)S(1)} %get-tuple-element.111), custom_call_target="InvertDiagBlocksLowerTriangular" | custom-call | tf_op jit(solution)/shard_map/triangular_solve/custom-call.4 | solution.py:86
  572.0 1.6 fusion.10
  575.8 9.3 %collective-permute-done.2 = f32[256,1,256]{2,0,1:T(8,128)S(1)} collective-permute-done((f32[256,1,256]{2,0,1:T(8,128)S(1)}, f32[256,1,256]{2,0,1:T(8,128)S(1)}, u32[]{:S(2)}, u32[]{:S(2)}) %collective-permute-start.2) | collective-permute-done | bytes 262176 | tf_op jit(solution)/shard_map/ppermute | solution.py:37
  585.1 1.8 collective-permute-start.3
  587.3 14.8 %collective-permute-done.3 = f32[256,1,256]{2,0,1:T(8,128)S(1)} collective-permute-done((f32[256,1,256]{2,0,1:T(8,128)S(1)}, f32[256,1,256]{2,0,1:T(8,128)S(1)}, u32[]{:S(2)}, u32[]{:S(2)}) %collective-permute-start.3) | collective-permute-done | bytes 262176 | tf_op jit(solution)/shard_map/ppermute | solution.py:37
  602.0 2.3 multiply_subtract_fusion
  604.3 2.0 copy.17
  (107 shorter events, 24.2 us)
Async XLA Ops:
  6.5 121.7 %reduce-scatter.3.cloned.1.call-start = ((), (), s32[]{:S(2)}) async-start(), calls=%async_computation.4 | async-start | bytes 1081344 | tf_op jit(solution)/shard_map/reduce_scatter | solution.py:20
  130.1 36.1 %all-to-all-start = ((f32[32,32,256]{2,1,0:T(8,128)}), f32[32,32,256]{2,1,0:T(8,128)S(1)}, u32[]{:S(2)}, u32[]{:S(2)}) async-start(f32[32,32,256]{2,1,0:T(8,128)} %stack.22), calls=%async_computation.1 | async-start | bytes 2097152 | tf_op jit(solution)/shard_map/all_to_all | solution.py:22
  138.2 81.3 %all-gather.5.cloned.1.call-start = ((), (), s32[]{:S(2)}) async-start(), calls=%async_computation.5 | async-start | bytes 2359296 | tf_op jit(solution)/shard_map/all_gather | solution.py:27
  167.0 114.6 %all-gather.7.cloned.1.call-start = ((), (), s32[]{:S(2)}) async-start(), calls=%async_computation.6 | async-start | bytes 2359296 | tf_op jit(solution)/shard_map/all_gather | solution.py:27
  167.8 233.0 %reduce-scatter.5.cloned.1.call-start = ((), (), s32[]{:S(2)}) async-start(), calls=%async_computation.7 | async-start | bytes 1081344 | tf_op jit(solution)/shard_map/reduce_scatter | solution.py:20
  402.7 37.1 %copy-start = (s32[2,4,256]{2,1,0:T(4,128)S(1)}, s32[2,4,256]{2,1,0:T(4,128)}, u32[]{:S(2)}) copy-start(s32[2,4,256]{2,1,0:T(4,128)} %param.21) | copy-start | bytes 24580
  402.7 37.1 %copy-start.1 = (s32[2,1,256]{2,1,0:T(1,128)S(1)}, s32[2,1,256]{2,1,0:T(1,128)}, u32[]{:S(2)}) copy-start(s32[2,1,256]{2,1,0:T(1,128)} %param.22) | copy-start | bytes 6148
  402.7 36.2 %all-to-all-start.1 = ((f32[32,32,256]{2,1,0:T(8,128)}), f32[32,32,256]{2,1,0:T(8,128)S(1)}, u32[]{:S(2)}, u32[]{:S(2)}) async-start(f32[32,32,256]{2,1,0:T(8,128)} %stack.28), calls=%async_computation.3 | async-start | bytes 2097152 | tf_op jit(solution)/shard_map/all_to_all | solution.py:22
  410.9 99.1 %all-gather.9.cloned.1.call-start = ((), (), s32[]{:S(2)}) async-start(), calls=%async_computation.8 | async-start | bytes 2359296 | tf_op jit(solution)/shard_map/all_gather | solution.py:27
  439.7 132.3 %all-gather.11.cloned.1.call-start = ((), (), s32[]{:S(2)}) async-start(), calls=%async_computation.9 | async-start | bytes 2359296 | tf_op jit(solution)/shard_map/all_gather | solution.py:27
  441.7 45.2 %collective-permute-start = (f32[1024,1,256]{2,0,1:T(8,128)}, f32[1024,1,256]{2,0,1:T(8,128)}, u32[]{:S(2)}, u32[]{:S(2)}) collective-permute-start(f32[1024,1,256]{2,0,1:T(8,128)} %bitcast_multiply_fusion), channel_id=1, source_target_pairs={{0,16},{16,0},{1,17},{17,1},{2,18},{18,2},{3,19},{19,3},{4,20},{20... | collective-permute-start | bytes 3145736 | tf_op jit(solution)/shard_map/ppermute | solution.py:37
  488.2 99.0 %collective-permute-start.1 = (f32[1024,1,256]{2,0,1:T(8,128)S(1)}, f32[1024,1,256]{2,0,1:T(8,128)}, u32[]{:S(2)}, u32[]{:S(2)}) collective-permute-start(f32[1024,1,256]{2,0,1:T(8,128)S(1)} %select_multiply_fusion), channel_id=1, source_target_pairs={{0,8},{8,0},{1,9},{9,1},{2,10},{10,2},{3,11},{11,3},{4,12},{12,4},... | collective-permute-start | bytes 3145736 | tf_op jit(solution)/shard_map/ppermute | solution.py:37
  575.4 9.7 %collective-permute-start.2 = (f32[256,1,256]{2,0,1:T(8,128)S(1)}, f32[256,1,256]{2,0,1:T(8,128)S(1)}, u32[]{:S(2)}, u32[]{:S(2)}) collective-permute-start(f32[256,1,256]{2,0,1:T(8,128)S(1)} %fusion.15), channel_id=1, source_target_pairs={{0,16},{16,0},{1,17},{17,1},{2,18},{18,2},{3,19},{19,3},{4,20},{20... | collective-permute-start | bytes 786440 | tf_op jit(solution)/shard_map/ppermute | solution.py:37
  585.1 16.9 %collective-permute-start.3 = (f32[256,1,256]{2,0,1:T(8,128)S(1)}, f32[256,1,256]{2,0,1:T(8,128)S(1)}, u32[]{:S(2)}, u32[]{:S(2)}) collective-permute-start(f32[256,1,256]{2,0,1:T(8,128)S(1)} %select_multiply_fusion.1), channel_id=1, source_target_pairs={{0,8},{8,0},{1,9},{9,1},{2,10},{10,2},{3,11},{11,3},{4,12},{12,4},... | collective-permute-start | bytes 786440 | tf_op jit(solution)/shard_map/ppermute | solution.py:37
Sparse Core Ops, SparseCore 0:
  11.4 116.7 reduce-scatter.2
  167.1 52.3 all-gather.4
  221.3 54.0 all-gather.6
  287.0 113.7 reduce-scatter.4
  439.8 70.1 all-gather.8
  511.6 50.8 all-gather.10
